TPU v7x, 32 devices: a 4x2x2 block of a 4x4x8 slice. The times are simulated.
32 devices in a mesh: dp: 4 (over y, z), sp: 8 (over x, core).
Axes of the slice: x: 4, y: 2, z: 2, core: 2. Of those that a mesh axis runs over, the one named last changes fastest.
The devices are a block of a 4x4x8 slice.
Arguments:
- hidden: bfloat16 [12288, 3072], P(('dp', 'sp')), parts along dimension 0
- positions: int32 [12288], P(('dp', 'sp')), parts along dimension 0
- norm_gain: bfloat16 [3072], replicated
- w_q: bfloat16 [3072, 3072], replicated
- b_q: bfloat16 [3072], replicated
- w_k: bfloat16 [3072, 1024], replicated
- b_k: bfloat16 [1024], replicated
- w_v: bfloat16 [3072, 1024], replicated
- b_v: bfloat16 [1024], replicated
- w_o: bfloat16 [3072, 3072], replicated
Outputs:
- output 1: bfloat16 [12288, 3072], P(('dp', 'sp')), parts along dimension 0
- output 2: bfloat16 [12288, 8, 128], P('dp', 'sp'), parts along dimension 0
- output 3: bfloat16 [12288, 8, 128], P('dp', 'sp'), parts along dimension 0
There are 4 independent parts. A program takes and returns all parts, laid end to end along the dimension named above; an argument that names none is the same for every part.
All inputs are finite; a program needn't handle non-finite values.
Results may differ from a plain program's by a relative error of at most 0.00856746.
Values are sent between devices in bfloat16 or wider.
A program may use at most 768 MiB of HBM per device.

v0:
```python
import math
import jax
import jax.numpy as jnp
from jax import lax
from jax.sharding import PartitionSpec as P

HEAD_DIM = 128
ROPE_BASE = 1000000.0
NORM_EPS = 1e-6


def rms_norm(hidden, norm_gain):
    wide = hidden.astype(jnp.float32)
    inv_rms = lax.rsqrt(jnp.mean(wide * wide, axis=-1, keepdims=True) + NORM_EPS)
    return (wide * inv_rms * norm_gain.astype(jnp.float32)).astype(jnp.bfloat16)


def project(normed, weight, bias):
    summed = jnp.dot(normed, weight, preferred_element_type=jnp.float32)
    return (summed + bias.astype(jnp.float32)).astype(jnp.bfloat16)


def apply_rope(heads, positions):
    half_dim = HEAD_DIM // 2
    inv_freq = ROPE_BASE ** (-2.0 * jnp.arange(half_dim, dtype=jnp.float32) / HEAD_DIM)
    angle = positions.astype(jnp.float32)[:, None, None] * inv_freq
    cosine = jnp.cos(angle)
    sine = jnp.sin(angle)
    wide = heads.astype(jnp.float32)
    lower = wide[..., :half_dim]
    upper = wide[..., half_dim:]
    turned = jnp.concatenate([lower * cosine - upper * sine, upper * cosine + lower * sine], axis=-1)
    return turned.astype(jnp.bfloat16)


def causal_attention(q_rows, k_all, v_all, block_starts, row_block, key_block):
    rows, groups, reps, head_dim = q_rows.shape
    scale = head_dim ** -0.5
    q_blocks = q_rows.reshape(rows // row_block, row_block, groups, reps, head_dim)
    row_offsets = jnp.arange(row_block)
    col_offsets = jnp.arange(key_block)

    def one_block(block_args):
        first_row, q_block = block_args
        row_ids = (first_row + row_offsets)[:, None, None, None]
        key_steps = (first_row + row_block + key_block - 1) // key_block

        def key_step(step_id, carry):
            run_max, run_sum, mixed = carry
            k_block = lax.dynamic_slice_in_dim(k_all, step_id * key_block, key_block, axis=0)
            v_block = lax.dynamic_slice_in_dim(v_all, step_id * key_block, key_block, axis=0)
            scores = jnp.einsum('qgrd,kgd->qgrk', q_block, k_block, preferred_element_type=jnp.float32) * scale
            col_ids = step_id * key_block + col_offsets
            scores = jnp.where(row_ids >= col_ids, scores, -jnp.inf)
            new_max = jnp.maximum(run_max, jnp.max(scores, axis=-1))
            rescale = jnp.exp(run_max - new_max)
            probs = jnp.exp(scores - new_max[..., None])
            run_sum = run_sum * rescale + jnp.sum(probs, axis=-1)
            mixed = mixed * rescale[..., None] + jnp.einsum('qgrk,kgd->qgrd', probs.astype(jnp.bfloat16), v_block, preferred_element_type=jnp.float32)
            return new_max, run_sum, mixed

        stat_shape = (row_block, groups, reps)
        start_carry = (jnp.full(stat_shape, -jnp.inf, jnp.float32), jnp.zeros(stat_shape, jnp.float32), jnp.zeros(stat_shape + (head_dim,), jnp.float32))
        run_max, run_sum, mixed = lax.fori_loop(0, key_steps, key_step, start_carry)
        return (mixed / run_sum[..., None]).astype(jnp.bfloat16)

    attended = lax.map(one_block, (block_starts, q_blocks))
    return attended.reshape(rows, groups, reps, head_dim)


def solution(mesh):
    group_size = mesh.shape['sp']
    row_spec = P(('dp', 'sp'), None)
    pos_spec = P(('dp', 'sp'))
    cache_spec = P('dp', 'sp', None)
    whole = P()

    def local(hidden, positions, norm_gain, w_q, b_q, w_k, b_k, w_v, b_v, w_o):
        tokens = hidden.shape[0]
        seq_len = tokens * group_size
        q_heads = w_q.shape[1] // HEAD_DIM
        kv_heads = w_k.shape[1] // HEAD_DIM
        reps = q_heads // kv_heads
        q_local = q_heads // group_size
        kv_local = kv_heads // group_size
        normed = rms_norm(hidden, norm_gain)
        queries = apply_rope(project(normed, w_q, b_q).reshape(tokens, q_heads, HEAD_DIM), positions)
        keys = apply_rope(project(normed, w_k, b_k).reshape(tokens, kv_heads, HEAD_DIM), positions)
        values = project(normed, w_v, b_v).reshape(tokens, kv_heads, HEAD_DIM)
        queries = lax.all_to_all(queries, 'sp', 1, 0, tiled=True)
        keys = lax.all_to_all(keys, 'sp', 1, 0, tiled=True)
        values = lax.all_to_all(values, 'sp', 1, 0, tiled=True)
        block = math.gcd(seq_len, 512)
        starts = jnp.arange(0, seq_len, block)
        attended = causal_attention(queries.reshape(seq_len, kv_local, reps, HEAD_DIM), keys, values, starts, block, block)
        attended = lax.all_to_all(attended.reshape(seq_len, q_local, HEAD_DIM), 'sp', 0, 1, tiled=True)
        summed = hidden.astype(jnp.float32) + jnp.dot(attended.reshape(tokens, q_heads * HEAD_DIM), w_o, preferred_element_type=jnp.float32)
        return summed.astype(jnp.bfloat16), keys, values

    return jax.shard_map(local, mesh=mesh, in_specs=(row_spec, pos_spec, whole, whole, whole, whole, whole, whole, whole, whole), out_specs=(row_spec, cache_spec, cache_spec), check_vma=False)
```

profile of v0, /device:TPU:81, one launch (start us, length us, event | category | flops | bytes accessed | tf_op | source)
XLA Modules:
  0.0 255.5 jit_solution(10983315319424086278)
XLA Ops:
  1.3 2.2 fusion.30
  4.2 6.2 %fusion.34 = bf16[48,8,8,128]{3,2,1,0:T(8,128)(2,1)S(1)} fusion(bf16[3072,1024]{1,0:T(8,128)(2,1)} %param.21, f32[1024]{0:T(1024)S(1)} %convert_element_type.75, bf16[384,3072]{1,0:T(8,128)(2,1)} %param.14, f32[3072]{0:T(1024)S(1)} %convert_element_type.64, f32[384]{0:T(512)S(1)} %add_rsqrt_fusion), kind=kOutput, calls=%fused_computation.52 | convolution fusion | flops 2421424128 | bytes 9455104 | tf_op jit(solution)/shard_map/dot_general | solution.py:19
  11.5 6.0 %all-to-all-start.2 = ((bf16[384,8,128]{2,0,1:T(8,128)(2,1)}), bf16[384,8,128]{2,0,1:T(8,128)(2,1)S(1)}, u32[]{:S(2)}, u32[]{:S(2)}) async-start(bf16[384,8,128]{2,0,1:T(8,128)(2,1)} %bitcast.97), calls=%async_computation.2 | async-start | bytes 1572864 | tf_op jit(solution)/shard_map/all_to_all | solution.py:92
  17.6 10.9 %convert_bitcast_fusion = f32[48,8,24,128]{3,1,2,0:T(8,128)S(1)} fusion(f32[3072]{0:T(1024)S(1)} %convert_element_type.66, bf16[3072,3072]{1,0:T(8,128)(2,1)} %param.17, bf16[384,3072]{1,0:T(8,128)(2,1)S(1)} %copy-done.2, f32[3072]{0:T(1024)S(1)} %convert_element_type.64, f32[384]{0:T(512)S(1)} %add_rsqrt_fusion), kind=kOutput, calls=%fused_computation.42 | convolution fusion | flops 7256014848 | bytes 25978368 | tf_op jit(solution)/shard_map/dot_general | solution.py:19
  29.5 1.5 fusion.38
  31.8 1.7 subtract_convert_fusion
  33.5 2.7 %pad_maximum_fusion = bf16[384,24,128]{2,0,1:T(8,128)(2,1)} fusion(bf16[384,24,64]{2,0,1:T(8,128)(2,1)S(1)} %get-tuple-element.345, bf16[384,24,64]{2,0,1:T(8,128)(2,1)S(1)} %get-tuple-element.344), kind=kLoop, calls=%fused_computation.46 | loop fusion | flops 4718592 | bytes 4718592 | tf_op jit(solution)/shard_map/concatenate | solution.py:32
  36.2 4.9 %all-to-all-start = ((bf16[384,24,128]{2,0,1:T(8,128)(2,1)}), bf16[384,24,128]{2,0,1:T(8,128)(2,1)S(1)}, u32[]{:S(2)}, u32[]{:S(2)}) async-start(bf16[384,24,128]{2,0,1:T(8,128)(2,1)} %pad_maximum_fusion), calls=%async_computation | async-start | bytes 4718592 | tf_op jit(solution)/shard_map/all_to_all | solution.py:90
  41.2 5.5 %convert_bitcast_fusion.1 = f32[48,8,8,128]{3,1,2,0:T(8,128)S(1)} fusion(bf16[3072,1024]{1,0:T(8,128)(2,1)} %param.19, f32[1024]{0:T(1024)S(1)} %convert_element_type.71, bf16[384,3072]{1,0:T(8,128)(2,1)} %param.14, f32[3072]{0:T(1024)S(1)} %convert_element_type.64, f32[384]{0:T(512)} %copy-done.6), kind=kOutput, calls=%fused_computation.47 | convolution fusion | flops 2421817344 | bytes 10241536 | tf_op jit(solution)/shard_map/dot_general | solution.py:19
  48.2 1.3 pad_maximum_fusion.1
  49.5 20.5 %all-to-all-done = bf16[384,24,128]{2,0,1:T(8,128)(2,1)S(1)} async-done(((bf16[384,24,128]{2,0,1:T(8,128)(2,1)}), bf16[384,24,128]{2,0,1:T(8,128)(2,1)S(1)}, u32[]{:S(2)}, u32[]{:S(2)}) %all-to-all-start) | async-done | bytes 2359328 | tf_op jit(solution)/shard_map/all_to_all | solution.py:90
  70.0 4.7 %all-to-all-start.1 = ((bf16[384,8,128]{2,0,1:T(8,128)(2,1)}), bf16[384,8,128]{2,0,1:T(8,128)(2,1)S(1)}, u32[]{:S(2)}, u32[]{:S(2)}) async-start(bf16[384,8,128]{2,0,1:T(8,128)(2,1)} %pad_maximum_fusion.1), calls=%async_computation.1 | async-start | bytes 1572864 | tf_op jit(solution)/shard_map/all_to_all | solution.py:91
  74.6 2.3 copy.46
  76.9 1.6 copy.41
  78.5 8.2 %all-to-all-done.1 = bf16[384,8,128]{2,0,1:T(8,128)(2,1)S(1)} async-done(((bf16[384,8,128]{2,0,1:T(8,128)(2,1)}), bf16[384,8,128]{2,0,1:T(8,128)(2,1)S(1)}, u32[]{:S(2)}, u32[]{:S(2)}) %all-to-all-start.1) | async-done | bytes 786464 | tf_op jit(solution)/shard_map/all_to_all | solution.py:91
  86.7 105.2 %while.67 = (s32[]{:T(128)}, bf16[6,512,1,3,128]{4,1,0,3,2:T(8,128)(2,1)}, s32[6]{0:T(128)S(1)}, bf16[6,512,1,3,128]{4,1,0,3,2:T(8,128)(2,1)}, bf16[3072,1,128]{...) while((s32[]{:T(128)}, ...), condition=%wide.region_6.7_spmd.clone.clone, body=%wide.region_1.6_spmd.clone.clone.sunk | while | flops 412358176 | bytes 17169564 | solution.py:67
  89.5 3.9 %while.68 = (s32[]{:T(128)}, f32[512,1,3]{0,2,1:T(4,128)S(1)}, f32[512,1,3]{0,2,1:T(4,128)S(1)}, f32[512,1,3,128]{0,3,2,1:T(8,128)S(1)}, s32[]{:T(128)}, /*index...) while((s32[]{:T(128)}, f32[512,1,3]{0,2,1:T(4,128)S(1)}, ...), condition=%wide.region_5.5_spmd, body=%wide.region_2.4_spmd.sunk | while | flops 411964416 | bytes 12820671 | solution.py:64
  90.5 2.1 fusion.58
  96.3 1.0 dynamic-slice_bitcast_fusion.2
  97.4 7.7 %while.68 = (s32[]{:T(128)}, f32[512,1,3]{0,2,1:T(4,128)S(1)}, f32[512,1,3]{0,2,1:T(4,128)S(1)}, f32[512,1,3,128]{0,3,2,1:T(8,128)S(1)}, s32[]{:T(128)}, /*index...) while((s32[]{:T(128)}, f32[512,1,3]{0,2,1:T(4,128)S(1)}, ...), condition=%wide.region_5.5_spmd, body=%wide.region_2.4_spmd.sunk | while | flops 411964416 | bytes 12820671 | solution.py:64
  98.4 2.1 fusion.58
  102.3 2.1 fusion.58
  109.2 11.6 %while.68 = (s32[]{:T(128)}, f32[512,1,3]{0,2,1:T(4,128)S(1)}, f32[512,1,3]{0,2,1:T(4,128)S(1)}, f32[512,1,3,128]{0,3,2,1:T(8,128)S(1)}, s32[]{:T(128)}, /*index...) while((s32[]{:T(128)}, f32[512,1,3]{0,2,1:T(4,128)S(1)}, ...), condition=%wide.region_5.5_spmd, body=%wide.region_2.4_spmd.sunk | while | flops 411964416 | bytes 12820671 | solution.py:64
  110.2 2.1 fusion.58
  114.0 2.1 fusion.58
  117.9 2.1 fusion.58
  124.8 15.4 %while.68 = (s32[]{:T(128)}, f32[512,1,3]{0,2,1:T(4,128)S(1)}, f32[512,1,3]{0,2,1:T(4,128)S(1)}, f32[512,1,3,128]{0,3,2,1:T(8,128)S(1)}, s32[]{:T(128)}, /*index...) while((s32[]{:T(128)}, f32[512,1,3]{0,2,1:T(4,128)S(1)}, ...), condition=%wide.region_5.5_spmd, body=%wide.region_2.4_spmd.sunk | while | flops 411964416 | bytes 12820671 | solution.py:64
  125.8 2.1 fusion.58
  129.6 2.1 fusion.58
  133.5 2.1 fusion.58
  137.3 2.1 fusion.58
  144.3 19.3 %while.68 = (s32[]{:T(128)}, f32[512,1,3]{0,2,1:T(4,128)S(1)}, f32[512,1,3]{0,2,1:T(4,128)S(1)}, f32[512,1,3,128]{0,3,2,1:T(8,128)S(1)}, s32[]{:T(128)}, /*index...) while((s32[]{:T(128)}, f32[512,1,3]{0,2,1:T(4,128)S(1)}, ...), condition=%wide.region_5.5_spmd, body=%wide.region_2.4_spmd.sunk | while | flops 411964416 | bytes 12820671 | solution.py:64
  145.3 2.1 fusion.58
  149.1 2.1 fusion.58
  153.0 2.1 fusion.58
  156.8 2.1 fusion.58
  160.7 2.1 fusion.58
  167.6 23.1 %while.68 = (s32[]{:T(128)}, f32[512,1,3]{0,2,1:T(4,128)S(1)}, f32[512,1,3]{0,2,1:T(4,128)S(1)}, f32[512,1,3,128]{0,3,2,1:T(8,128)S(1)}, s32[]{:T(128)}, /*index...) while((s32[]{:T(128)}, f32[512,1,3]{0,2,1:T(4,128)S(1)}, ...), condition=%wide.region_5.5_spmd, body=%wide.region_2.4_spmd.sunk | while | flops 411964416 | bytes 12820671 | solution.py:64
  168.6 2.1 fusion.58
  172.4 2.1 fusion.58
  176.3 2.1 fusion.58
  180.1 2.1 fusion.58
  184.0 2.1 fusion.58
  187.8 2.1 fusion.58
  191.9 4.3 %copy.48 = bf16[3072,3,128]{2,1,0:T(4,128)(2,1)S(1)} copy(bf16[3072,3,128]{2,0,1:T(8,128)(2,1)} %bitcast.144) | data formatting | bytes 4718592 | tf_op jit(solution)/shard_map/reshape;reshape | solution.py:96
  196.2 41.1 %all_to_all.66 = bf16[3072,3,128]{2,1,0:T(4,128)(2,1)S(1)} all-to-all(bf16[3072,3,128]{2,1,0:T(4,128)(2,1)S(1)} %copy.48), channel_id=1, replica_groups=mesh['dp'=4,'sp'=8] {'sp'}, dimensions={0} | all-to-all | bytes 4718592 | tf_op jit(solution)/shard_map/all_to_all | solution.py:96
  237.7 2.5 copy.50
  240.2 13.5 %fusion.33 = bf16[384,3072]{1,0:T(8,128)(2,1)} fusion(bf16[384,3072]{1,0:T(8,128)(2,1)} %param.14, bf16[384,3072]{0,1:T(8,128)(2,1)} %bitcast.143, bf16[3072,3072]{1,0:T(8,128)(2,1)} %param.23), kind=kOutput, calls=%fused_computation.41 | convolution fusion | flops 7251296256 | bytes 25952256 | tf_op jit(solution)/shard_map/dot_general | solution.py:97
  (239 shorter events, 61.7 us)
Async XLA Ops:
  3.5 14.0 %copy-start.6 = (f32[384]{0:T(512)}, f32[384]{0:T(512)S(1)}, u32[]{:S(2)}) copy-start(f32[384]{0:T(512)S(1)} %add_rsqrt_fusion) | copy-start | bytes 4612
  10.4 7.1 %copy-start.5 = (s32[384]{0:T(512)S(1)}, s32[384]{0:T(512)}, u32[]{:S(2)}) copy-start(s32[384]{0:T(512)} %param.15) | copy-start | bytes 4612
  10.5 7.1 %copy-start.3 = (bf16[3072]{0:T(1024)(128)(2,1)S(1)}, bf16[3072]{0:T(1024)(128)(2,1)}, u32[]{:S(2)}) copy-start(bf16[3072]{0:T(1024)(128)(2,1)} %param.18) | copy-start | bytes 18436
  10.5 7.1 %copy-start.2 = (bf16[384,3072]{1,0:T(8,128)(2,1)S(1)}, bf16[384,3072]{1,0:T(8,128)(2,1)}, u32[]{:S(2)}) copy-start(bf16[384,3072]{1,0:T(8,128)(2,1)} %param.14) | copy-start | bytes 7077892
  11.5 24.7 %all-to-all-start.2 = ((bf16[384,8,128]{2,0,1:T(8,128)(2,1)}), bf16[384,8,128]{2,0,1:T(8,128)(2,1)S(1)}, u32[]{:S(2)}, u32[]{:S(2)}) async-start(bf16[384,8,128]{2,0,1:T(8,128)(2,1)} %bitcast.97), calls=%async_computation.2 | async-start | bytes 1572864 | tf_op jit(solution)/shard_map/all_to_all | solution.py:92
  36.2 5.0 %copy-start.4 = (bf16[1024]{0:T(1024)(128)(2,1)S(1)}, bf16[1024]{0:T(1024)(128)(2,1)}, u32[]{:S(2)}) copy-start(bf16[1024]{0:T(1024)(128)(2,1)} %param.20) | copy-start | bytes 6148
  36.2 10.5 %copy-start = (bf16[384,8,128]{2,0,1:T(8,128)(2,1)}, bf16[384,8,128]{2,0,1:T(8,128)(2,1)S(1)}, u32[]{:S(2)}) copy-start(bf16[384,8,128]{2,0,1:T(8,128)(2,1)S(1)} %all-to-all-done.2) | copy-start | bytes 2359300
  36.2 33.7 %all-to-all-start = ((bf16[384,24,128]{2,0,1:T(8,128)(2,1)}), bf16[384,24,128]{2,0,1:T(8,128)(2,1)S(1)}, u32[]{:S(2)}, u32[]{:S(2)}) async-start(bf16[384,24,128]{2,0,1:T(8,128)(2,1)} %pad_maximum_fusion), calls=%async_computation | async-start | bytes 4718592 | tf_op jit(solution)/shard_map/all_to_all | solution.py:90
  70.0 16.7 %all-to-all-start.1 = ((bf16[384,8,128]{2,0,1:T(8,128)(2,1)}), bf16[384,8,128]{2,0,1:T(8,128)(2,1)S(1)}, u32[]{:S(2)}, u32[]{:S(2)}) async-start(bf16[384,8,128]{2,0,1:T(8,128)(2,1)} %pad_maximum_fusion.1), calls=%async_computation.1 | async-start | bytes 1572864 | tf_op jit(solution)/shard_map/all_to_all | solution.py:91
  240.2 14.4 %copy-start.1 = (bf16[384,8,128]{2,0,1:T(8,128)(2,1)S(1)}, bf16[384,8,128]{2,0,1:T(8,128)(2,1)}, u32[]{:S(2)}) copy-start(bf16[384,8,128]{2,0,1:T(8,128)(2,1)} %copy-done) | copy-start | bytes 2359300
where the time goes:
time: 257 us; the launch traced here: 255 us
  matrix products  95.6 us (37%)
  blocking collectives  41.1 us (16%)
  other arithmetic  34.5 us (13%)
  local copies, waits for them, and re-layouts  33.7 us (13%)
  waiting for transfers between devices  28.6 us (11%)
  starting transfers between devices  15.6 us (6%)
  loops' own time  5.46 us (2%)
    dot_general x21, matrix products, key_step(): jnp.einsum('qgrk,kgd->qgrd', probs.astype(jnp.bfloat16), v_block, preferr...  44.8 us
    all_to_all x1, blocking collectives, local(): lax.all_to_all(attended.reshape(seq_len, q_local, HEAD_DIM), 'sp', 0, 1,...  41.1 us
    dot_general x3, matrix products, project(): summed = jnp.dot(normed, weight, preferred_element_type=jnp.float32)  22.6 us
    all_to_all x1, waiting for transfers between devices, local(): queries = lax.all_to_all(queries, 'sp', 1, 0, tiled=True)  20.5 us
    reduce_sum x21, other arithmetic, key_step(): run_sum = run_sum * rescale + jnp.sum(probs, axis=-1)  14.7 us
    dot_general x21, matrix products, key_step(): jnp.einsum('qgrd,kgd->qgrk', q_block, k_block, preferred_element_type=jnp...  14.7 us
    dot_general x1, matrix products, local(): jnp.dot(attended.reshape(tokens, q_heads * HEAD_DIM), w_o, preferred_elem...  13.5 us
    all_to_all x1, waiting for transfers between devices, local(): keys = lax.all_to_all(keys, 'sp', 1, 0, tiled=True)  8.18 us
  transfers between devices with their start and end apart: 3, of which 2 were waited for; matrix products, arithmetic and copies ran while one was open for 12% of the time, Pallas kernels for 0%

commit v1 on v0

v1 whole, which is shorter than its diff:
```python
import functools
import math

import jax
import jax.numpy as jnp
from jax import lax
from jax.experimental import pallas as pl
from jax.experimental.pallas import tpu as pltpu
from jax.sharding import PartitionSpec as P

HEAD_DIM = 128
ROPE_BASE = 1000000.0
NORM_EPS = 1e-6
SCORE_SCALE = math.log2(math.e) / math.sqrt(HEAD_DIM)
CHIPS = 4
GROUPS = 4
REPS = 3
TILE = 256
BF16 = jnp.bfloat16
F32 = jnp.float32


def rope_tables(positions):
    half_dim = HEAD_DIM // 2
    inv_freq = ROPE_BASE ** (-2.0 * jnp.arange(half_dim, dtype=F32) / HEAD_DIM)
    angle = positions.astype(F32)[:, None] * inv_freq
    cosine = jnp.cos(angle)
    sine = jnp.sin(angle)
    return jnp.concatenate([cosine, cosine], axis=-1), jnp.concatenate([-sine, sine], axis=-1)


def matmul(a, b):
    return lax.dot_general(a, b, (((1,), (0,)), ((), ())), preferred_element_type=F32)


def matmul_t(a, b):
    return lax.dot_general(a, b, (((1,), (1,)), ((), ())), preferred_element_type=F32)


def lane_blocks(x):
    return [x[:, i : i + 128] for i in range(0, x.shape[1], 128)]


def pipelined(count, score, soft, mix):
    scores, weights = {}, {}
    for t in range(count + 2):
        if t < count:
            scores[t] = score(t)
        if 0 <= t - 1 < count:
            weights[t - 1] = soft(t - 1, scores.pop(t - 1))
        if 0 <= t - 2 < count:
            mix(t - 2, *weights.pop(t - 2))


def kernel(
    x_hbm, cos_ref, sin_ref, gain_ref, bq_ref, bk_ref, bv_ref, wq_hbm, wk_hbm, wv_hbm, wo_hbm,
    y_hbm, kc_hbm, vc_hbm,
    xbuf, hbuf, wkv, wbuf, kv, kst, qbuf, qst, run_max, run_sum, mixed, obuf, ost,
    xsem, wkvsem, wqsem, wosem, ysem, csem,
    kv_recv, kv_send, q_recv, q_send, o_recv, o_send, fwd_send,
):
    me = lax.axis_index("sp")
    chip = lax.div(me, 2)
    core = lax.rem(me, 2)
    other = 1 - core
    up = lax.rem(chip + 1, CHIPS)
    down = lax.rem(chip + CHIPS - 1, CHIPS)
    tokens = xbuf.shape[0]
    block = 2 * tokens
    my_rows = pl.ds(pl.multiple_of(core * tokens, 128), tokens)
    other_rows = pl.ds(pl.multiple_of(other * tokens, 128), tokens)

    def is_chip(n):
        return chip == n

    def device(on_chip, on_core):
        return {"sp": on_chip * 2 + on_core}

    def remote(src, dst, send_sem, recv_sem, on_chip, on_core):
        return pltpu.make_async_remote_copy(
            src_ref=src, dst_ref=dst, send_sem=send_sem, recv_sem=recv_sem,
            device_id=device(on_chip, on_core), device_id_type=pl.DeviceIdType.MESH,
        )

    barrier = pltpu.get_barrier_semaphore()
    for on_chip, on_core in ((chip, other), (up, core), (up, other), (down, core), (down, other)):
        pl.semaphore_signal(barrier, inc=1, device_id=device(on_chip, on_core), device_id_type=pl.DeviceIdType.MESH)

    first_group = jnp.where(chip == 0, 0, 1)

    def group_at(i):
        return lax.rem(i + first_group, GROUPS)

    def kv_load(chunk_i, kind):
        w_hbm = wk_hbm if kind == 0 else wv_hbm
        chunk = 2 * chunk_i + kind
        cols = pl.ds(pl.multiple_of(group_at(chunk_i) * 256, 256), 256)
        return pltpu.make_async_copy(w_hbm.at[:, cols], wkv.at[lax.rem(chunk, 4)], wkvsem.at[chunk])

    def wide_load(w_hbm, g, sem):
        cols = pl.ds(pl.multiple_of(g * 768, 256), 768)
        return pltpu.make_async_copy(w_hbm.at[:, cols], wbuf.at[g], sem.at[g])

    x_copy = pltpu.make_async_copy(x_hbm, xbuf, xsem)
    x_copy.start()
    for i in range(2):
        for kind in range(2):
            kv_load(jnp.int32(i), kind).start()
    x_copy.wait()

    @pl.loop(0, tokens // 32)
    def _(i):
        rows = pl.ds(pl.multiple_of(i * 32, 32), 32)
        wide = xbuf[rows, :].astype(F32)
        inv_rms = lax.rsqrt(jnp.mean(wide * wide, axis=-1, keepdims=True) + NORM_EPS)
        hbuf[rows, :] = (wide * inv_rms * gain_ref[...]).astype(BF16)

    pl.semaphore_wait(barrier, 5)

    def rope(u):
        wide = u.astype(F32)
        return (wide * cos_ref[...] + pltpu.roll(wide, HEAD_DIM // 2, 1) * sin_ref[...]).astype(BF16)

    def goes_partner(g):
        return jnp.logical_not((chip == 3) & (g == 0))

    def goes_up(g):
        return (chip <= 1) | ((chip == 2) & (g >= 1)) | ((chip == 3) & (g <= 1))

    def goes_down(g):
        return ((chip == 0) & (g >= 1)) | ((chip == 1) & ((g == 0) | (g == 3))) | ((chip == 2) & (g <= 1)) | ((chip == 3) & (g == 2))

    def own_copies(g):
        dst = kv.at[chip, g, :, my_rows, :]
        recv = kv_recv.at[chip, g, core]
        yield goes_partner(g), [remote(kst.at[g], dst, kv_send.at[g, 0], recv, chip, other)]
        yield goes_up(g), [
            remote(dst, dst, kv_send.at[g, 1], recv, up, core), remote(kst.at[g], dst, kv_send.at[g, 2], recv, up, other)]
        yield goes_down(g), [
            remote(dst, dst, kv_send.at[g, 3], recv, down, core), remote(kst.at[g], dst, kv_send.at[g, 4], recv, down, other)]

    def each(copies, act):
        for go, group in copies:
            @pl.when(go)
            def _():
                for copy in group:
                    act(copy)

    @pl.loop(0, GROUPS)
    def _(i):
        g = group_at(i)
        cols = pl.ds(pl.multiple_of(g * 256, 256), 256)
        for kind, b_ref in ((0, bk_ref), (1, bv_ref)):
            chunk = 2 * i + kind
            kv_load(i, kind).wait()
            u = (matmul(hbuf[...], wkv[lax.rem(chunk, 4)]) + b_ref[:, cols]).astype(BF16)
            even, odd = lane_blocks(u)
            if kind == 0:
                even, odd = rope(even), rope(odd)
            kv[chip, g, kind, my_rows, :] = jnp.where(core == 0, even, odd)
            kst[g, kind] = jnp.where(core == 0, odd, even)

            @pl.when(i < 2)
            def _():
                kv_load(i + 2, kind).start()

        wide_load(wq_hbm, i, wqsem).start()
        each(own_copies(g), lambda copy: copy.start())

    def q_copies(g):
        mine = qbuf.at[g, :, my_rows, :]
        away = (chip == 3) & (g == 0)
        yield jnp.logical_not(away), [
            remote(qst.at[g], mine, q_send.at[g, 0], q_recv.at[g, core], chip, other)]
        there = qbuf.at[GROUPS, :, my_rows, :]
        yield away, [
            remote(mine, there, q_send.at[g, 1], q_recv.at[GROUPS, core], up, core),
            remote(qst.at[g], there, q_send.at[g, 0], q_recv.at[GROUPS, core], up, other)]

    @pl.loop(0, GROUPS)
    def _(g):
        wide_load(wq_hbm, g, wqsem).wait()
        heads = []
        for n in range(3):
            cols = pl.ds(pl.multiple_of(g * 768 + n * 256, 256), 256)
            u = (matmul(hbuf[...], wbuf[g, :, n * 256 : (n + 1) * 256]) + bq_ref[:, cols]).astype(BF16)
            heads += [rope(part) for part in lane_blocks(u)]
        for r in range(REPS):
            even, odd = heads[r], heads[REPS + r]
            qbuf[g, r, my_rows, :] = jnp.where(core == 0, even, odd)
            qst[g, r] = jnp.where(core == 0, odd, even)
        wide_load(wo_hbm, g, wosem).start()
        each(q_copies(g), lambda copy: copy.start())

    def wait_straight(s, g):
        for j in range(2):
            part = kv.at[s, g, :, pl.ds(j * tokens, tokens), :]
            pltpu.make_async_copy(part, part, kv_recv.at[s, g, j]).wait()

    def wait_passed(s, g):
        pltpu.make_async_copy(kv.at[s, g], kv.at[s, g], kv_recv.at[s, g, 0]).wait()

    def pass_on(s, g, to_chip, slot):
        return remote(kv.at[s, g], kv.at[s, g], fwd_send.at[slot], kv_recv.at[s, g, 0], to_chip, core)

    q_tiles = block // TILE

    def tile_rows(t):
        return t // q_tiles, slice((t % q_tiles) * TILE, (t % q_tiles + 1) * TILE)

    def masked_item(q_slot, slot, s, g):
        def score(t):
            r, rows = tile_rows(t)
            sc = matmul_t(qbuf[q_slot, r, rows, :], kv[s, g, 0, 0 : rows.stop, :])
            seen = lax.broadcasted_iota(jnp.int32, (TILE, TILE), 0) >= lax.broadcasted_iota(jnp.int32, (TILE, TILE), 1)
            last = jnp.where(seen, sc[:, rows.start :], -jnp.inf)
            return last if rows.start == 0 else jnp.concatenate([sc[:, : rows.start], last], axis=1)

        def soft(t, sc):
            r, rows = tile_rows(t)
            parts = lane_blocks(sc)
            top = functools.reduce(jnp.maximum, parts)
            top = jnp.broadcast_to(jnp.max(top, axis=1, keepdims=True) * SCORE_SCALE, (TILE, 128))
            probs = [jnp.exp2(part * SCORE_SCALE - top) for part in parts]
            run_max[slot, r, rows, :] = top
            run_sum[slot, r, rows, :] = functools.reduce(jnp.add, probs)
            return (jnp.concatenate([p.astype(BF16) for p in probs], axis=1),)

        def mix(t, probs):
            r, rows = tile_rows(t)
            mixed[slot, r, rows, :] = matmul(probs, kv[s, g, 1, 0 : rows.stop, :])

        pipelined(REPS * q_tiles, score, soft, mix)

    def full_item(q_slot, slot, s, g):
        def score(t):
            r, rows = tile_rows(t)
            return matmul_t(qbuf[q_slot, r, rows, :], kv[s, g, 0])

        def soft(t, sc):
            r, rows = tile_rows(t)
            parts = lane_blocks(sc)
            before = run_max[slot, r, rows, :]
            top = functools.reduce(jnp.maximum, parts)
            top = jnp.maximum(before, jnp.max(top, axis=1, keepdims=True) * SCORE_SCALE)
            rescale = jnp.exp2(before - top)
            probs = [jnp.exp2(part * SCORE_SCALE - top) for part in parts]
            run_max[slot, r, rows, :] = top
            run_sum[slot, r, rows, :] = run_sum[slot, r, rows, :] * rescale + functools.reduce(jnp.add, probs)
            return jnp.concatenate([p.astype(BF16) for p in probs], axis=1), rescale

        def mix(t, probs, rescale):
            r, rows = tile_rows(t)
            mixed[slot, r, rows, :] = mixed[slot, r, rows, :] * rescale + matmul(probs, kv[s, g, 1])

        pipelined(REPS * q_tiles, score, soft, mix)

    def head_cols(g, parity):
        return pl.ds(pl.multiple_of((2 * g + parity) * REPS * 128, 128), REPS * 128)

    def normalized(slot, r, rows):
        total = jnp.sum(run_sum[slot, r, rows, :], axis=1, keepdims=True)
        return (mixed[slot, r, rows, :] / total).astype(BF16)

    def o_copy(g):
        return remote(ost.at[g], obuf.at[:, head_cols(g, core)], o_send.at[g], o_recv.at[g, core], chip, other)

    def finish(g):
        for r in range(REPS):
            ost[g, :, r * 128 : (r + 1) * 128] = normalized(g, r, other_rows)
        o_copy(g).start()
        for r in range(REPS):
            cols = pl.ds(pl.multiple_of(((2 * g + core) * REPS + r) * 128, 128), 128)
            obuf[:, cols] = normalized(g, r, my_rows)

    def back_copies():
        for j in range(2):
            yield remote(ost.at[GROUPS + j], obuf.at[:, head_cols(0, core)], o_send.at[GROUPS + j], o_recv.at[0, core], down, j)

    low = jnp.where(chip == 3, 1, 0)

    @pl.loop(low, jnp.where(chip == 0, GROUPS + 1, GROUPS))
    def _(i):
        g = lax.rem(i, GROUPS)

        @pl.when(i < GROUPS)
        def _():
            part = qbuf.at[i, :, other_rows, :]
            pltpu.make_async_copy(part, part, q_recv.at[i, other]).wait()
            part = kv.at[chip, g, :, other_rows, :]
            pltpu.make_async_copy(part, part, kv_recv.at[chip, g, other]).wait()

        @pl.when(i == GROUPS)
        def _():
            wait_straight(1, 3)
            pass_on(1, 3, 3, 0).start()
            wait_straight(3, 1)
            pass_on(3, 1, 1, 1).start()
            wait_straight(3, 0)
            for j in range(2):
                part = qbuf.at[GROUPS, :, pl.ds(j * tokens, tokens), :]
                pltpu.make_async_copy(part, part, q_recv.at[GROUPS, j]).wait()

        masked_item(i, g, jnp.where(i == GROUPS, 3, chip), g)

        @pl.when((chip == 0) & (i < GROUPS))
        def _():
            finish(i)

    straight = jnp.where(chip == 0, 3, jnp.where(chip == 3, 6, 4))
    items = straight + jnp.where(chip == 3, 3, jnp.where(chip == 2, 4, 0))

    @pl.loop(0, items)
    def _(i):
        late = i - straight
        in_order = lax.rem(i, GROUPS)
        shifted = lax.rem(i + 1, GROUPS)
        s = jnp.where(
            chip == 0, i,
            jnp.where(chip == 1, 0,
                jnp.where(chip == 2, jnp.where(late < 0, 1, 0), jnp.where(late < 0, 2 - 2 * lax.rem(i, 2), 1))))
        g = jnp.where(
            chip == 0, 0,
            jnp.where(chip == 1, in_order,
                jnp.where(chip == 2, shifted, jnp.where(late < 0, 1 + lax.div(i, 2), 1 + lax.rem(2 * late + 6, 3)))))
        q_slot = jnp.where(chip == 0, GROUPS, g)
        is_passed = ((chip == 0) & (i == 2)) | (late >= 0)
        is_local = (chip == 0) & (i == 0)

        @pl.when(is_passed)
        def _():
            wait_passed(s, g)

        @pl.when(jnp.logical_not(is_passed | is_local))
        def _():
            wait_straight(s, g)

        @pl.when((chip == 1) & (i == 0))
        def _():
            pass_on(0, 0, 2, 0).start()

        @pl.when((chip == 1) & (i == 1))
        def _():
            wait_straight(2, 0)
            pass_on(2, 0, 0, 1).start()

        @pl.when((chip == 2) & (late < 0) & ((g == 1) | (g == 2)))
        def _():
            pass_on(1, g, 3, g - 1).start()

        @pl.when((chip == 3) & (late < 0) & (s == 0))
        def _():
            pass_on(0, g, 2, g - 1).start()

        full_item(q_slot, g, s, g)

    @pl.when(chip == 0)
    def _():
        for j in range(2):
            rows = pl.ds(j * tokens, tokens)
            for r in range(REPS):
                ost[GROUPS + j, :, r * 128 : (r + 1) * 128] = normalized(0, r, rows)
        for copy in back_copies():
            copy.start()

    @pl.when(chip > 0)
    def _():
        @pl.loop(low, GROUPS)
        def _(g):
            finish(g)

    @pl.when(chip == 1)
    def _():
        wait_straight(2, 1)
        wait_passed(3, 1)

    @pl.when(chip == 2)
    def _():
        wait_straight(3, 2)

    cache_copies = []
    for s in range(CHIPS):
        for kind, c_hbm in ((0, kc_hbm), (1, vc_hbm)):
            cache_copies.append(
                pltpu.make_async_copy(kv.at[s, chip, kind], c_hbm.at[pl.ds(s * block, block), :], csem.at[s, kind]))
    for copy in cache_copies:
        copy.start()

    def wait_o(g, parity):
        part = obuf.at[:, head_cols(g, parity)]
        pltpu.make_async_copy(part, part, o_recv.at[g, parity]).wait()

    @pl.loop(low, GROUPS)
    def _(g):
        wait_o(g, other)

    @pl.when(chip == 3)
    def _():
        for parity in range(2):
            wait_o(0, parity)

    def y_copy(n):
        cols = pl.ds(pl.multiple_of(n * 768, 256), 768)
        return pltpu.make_async_copy(xbuf.at[:, cols], y_hbm.at[:, cols], ysem.at[n])

    @pl.loop(0, 4)
    def _(n):
        wide_load(wo_hbm, n, wosem).wait()
        for part in range(3):
            cols = pl.ds(pl.multiple_of(n * 768 + part * 256, 256), 256)
            summed = matmul(obuf[...], wbuf[n, :, part * 256 : (part + 1) * 256])
            xbuf[:, cols] = (xbuf[:, cols].astype(F32) + summed).astype(BF16)
        y_copy(n).start()

    @pl.loop(0, GROUPS)
    def _(g):
        each(own_copies(g), lambda copy: copy.wait_send())
        each(q_copies(g), lambda copy: copy.wait_send())

    @pl.loop(low, GROUPS)
    def _(g):
        o_copy(g).wait_send()

    @pl.when(chip == 0)
    def _():
        for copy in back_copies():
            copy.wait_send()

    for slot in range(2):
        pass_on(0, 0, up, slot).wait_send()

    @pl.when(chip == 3)
    def _():
        pass_on(0, 0, up, 2).wait_send()

    for copy in cache_copies:
        copy.wait()

    @pl.loop(0, 4)
    def _(n):
        y_copy(n).wait()


def solution(mesh):
    group_size = mesh.shape['sp']
    row_spec = P(('dp', 'sp'), None)
    pos_spec = P(('dp', 'sp'))
    cache_spec = P('dp', 'sp', None)
    whole = P()

    def local(hidden, positions, norm_gain, w_q, b_q, w_k, b_k, w_v, b_v, w_o):
        tokens, width = hidden.shape
        block = 2 * tokens
        seq_len = tokens * group_size
        cosine, sine = rope_tables(positions)
        vmem = pl.BlockSpec(memory_space=pltpu.VMEM)
        anywhere = pl.BlockSpec(memory_space=pl.ANY)
        dma = pltpu.SemaphoreType.DMA
        y, keys, values = pl.pallas_call(
            kernel,
            out_shape=[
                jax.ShapeDtypeStruct((tokens, width), BF16),
                jax.ShapeDtypeStruct((seq_len, HEAD_DIM), BF16),
                jax.ShapeDtypeStruct((seq_len, HEAD_DIM), BF16),
            ],
            in_specs=[anywhere] + [vmem] * 6 + [anywhere] * 4,
            out_specs=[anywhere] * 3,
            scratch_shapes=[
                pltpu.VMEM((tokens, width), BF16),
                pltpu.VMEM((tokens, width), BF16),
                pltpu.VMEM((4, width, 256), BF16),
                pltpu.VMEM((GROUPS, width, 768), BF16),
                pltpu.VMEM((CHIPS, GROUPS, 2, block, HEAD_DIM), BF16),
                pltpu.VMEM((GROUPS, 2, tokens, HEAD_DIM), BF16),
                pltpu.VMEM((GROUPS + 1, REPS, block, HEAD_DIM), BF16),
                pltpu.VMEM((GROUPS, REPS, tokens, HEAD_DIM), BF16),
                pltpu.VMEM((GROUPS, REPS, block, HEAD_DIM), F32),
                pltpu.VMEM((GROUPS, REPS, block, HEAD_DIM), F32),
                pltpu.VMEM((GROUPS, REPS, block, HEAD_DIM), F32),
                pltpu.VMEM((tokens, width), BF16),
                pltpu.VMEM((GROUPS + 2, tokens, REPS * HEAD_DIM), BF16),
                dma, dma((8,)), dma((4,)), dma((4,)), dma((4,)), dma((CHIPS, 2)),
                dma((CHIPS, GROUPS, 2)), dma((GROUPS, 5)), dma((GROUPS + 1, 2)), dma((GROUPS, 2)),
                dma((GROUPS, 2)), dma((GROUPS + 2,)), dma((3,)),
            ],
            compiler_params=pltpu.CompilerParams(
                collective_id=0, has_side_effects=True, vmem_limit_bytes=67043328),
            name="block",
        )(
            hidden, cosine, sine, norm_gain.astype(F32)[None], b_q.astype(F32)[None], b_k.astype(F32)[None],
            b_v.astype(F32)[None], w_q, w_k, w_v, w_o,
        )
        return y, keys[:, None, :], values[:, None, :]

    return jax.shard_map(local, mesh=mesh, in_specs=(row_spec, pos_spec, whole, whole, whole, whole, whole, whole, whole, whole), out_specs=(row_spec, cache_spec, cache_spec), check_vma=False)
```

time: 257 us -> 95 us (0.37)
  the two profiles are of different devices: /device:TPU:81 before, /device:TPU:125 now
where the time goes in v1:
time: 95 us; the launch traced here: 94.7 us
  Pallas kernels  80.3 us (85%)
  other arithmetic  7.51 us (8%)
  local copies, waits for them, and re-layouts  6.24 us (7%)
    pallas_call x1, Pallas kernels, local(): pl.pallas_call(kernel, out_shape=[jax.ShapeDtypeStruct((tokens, width), B...  80.3 us
    unnamed x5, local copies, waits for them, and re-layouts  6.24 us

profile of v1, /device:TPU:125, one launch (start us, length us, event | category | flops | bytes accessed | tf_op | source)
XLA Modules:
  0.0 94.7 jit_solution(96001954511543737)
XLA Ops:
  0.6 0.7 convert_element_type.2
  1.3 1.3 %broadcast_in_dim.40 = f32[1024]{0:T(1024)} convert(bf16[1024]{0:T(1024)(128)(2,1)} %param.16) | non-fusion elementwise | flops 1024 | bytes 6144 | tf_op jit(solution)/shard_map/broadcast_in_dim | solution.py:490
  2.6 1.3 %broadcast_in_dim.41 = f32[1024]{0:T(1024)} convert(bf16[1024]{0:T(1024)(128)(2,1)} %param.18) | non-fusion elementwise | flops 1024 | bytes 6144 | tf_op jit(solution)/shard_map/broadcast_in_dim | solution.py:491
  3.9 1.3 %broadcast_in_dim.38 = f32[3072]{0:T(1024)} convert(bf16[3072]{0:T(1024)(128)(2,1)} %param.12) | non-fusion elementwise | flops 3072 | bytes 18432 | tf_op jit(solution)/shard_map/broadcast_in_dim | solution.py:490
  5.2 1.3 %broadcast_in_dim.39 = f32[3072]{0:T(1024)} convert(bf16[3072]{0:T(1024)(128)(2,1)} %param.14) | non-fusion elementwise | flops 3072 | bytes 18432 | tf_op jit(solution)/shard_map/broadcast_in_dim | solution.py:490
  6.5 0.8 fusion
  7.2 0.9 pad_maximum_fusion
  8.2 80.3 %block.1 = (bf16[384,3072]{1,0:T(8,128)(2,1)}, bf16[3072,128]{1,0:T(8,128)(2,1)}, bf16[3072,128]{1,0:T(8,128)(2,1)}) custom-call(bf16[384,3072]{1,0:T(8,128)(2,1)} %x_hbm.1, f32[384,128]{1,0:T(8,128)} %get-tuple-element.12.cos_ref, f32[384,128]{1,0:T(8,128)} %get-tuple-element.13.sin_ref, f32[1,3072]{1,0:T(1,128)} %bitcast.8, f32[1,3072]{1,0:T(1,128)} %bitcast.9, ...), custom_call_target="tpu_custom_call" | custom-call | tf_op jit(solution)/shard_map/block/pallas_call | solution.py:459
  88.4 0.0 copy-start
  88.5 3.3 %copy.16 = bf16[384,3072]{1,0:T(8,128)(2,1)} copy(bf16[384,3072]{1,0:T(8,128)(2,1)} %get-tuple-element.17) | data formatting | bytes 4718592
  91.8 2.1 %copy.17 = bf16[3072,1,128]{2,0,1:T(8,128)(2,1)} copy(bf16[3072,1,128]{2,0,1:T(8,128)(2,1)} %bitcast.7) | data formatting | bytes 1572864
  93.8 0.0 copy-done
  93.8 0.9 copy.18
  (1 shorter events, 0.0 us)
Async XLA Ops:
  88.4 5.4 %copy-start = (bf16[3072,128]{1,0:T(8,128)(2,1)S(1)}, bf16[3072,128]{1,0:T(8,128)(2,1)}, u32[]{:S(2)}) copy-start(bf16[3072,128]{1,0:T(8,128)(2,1)} %get-tuple-element.8) | copy-start | bytes 2359300

commit v2 on v1

--- a/solution.py
+++ b/solution.py
@@ -24,9 +24,7 @@
     half_dim = HEAD_DIM // 2
     inv_freq = ROPE_BASE ** (-2.0 * jnp.arange(half_dim, dtype=F32) / HEAD_DIM)
     angle = positions.astype(F32)[:, None] * inv_freq
-    cosine = jnp.cos(angle)
-    sine = jnp.sin(angle)
-    return jnp.concatenate([cosine, cosine], axis=-1), jnp.concatenate([-sine, sine], axis=-1)
+    return jnp.cos(angle), jnp.sin(angle)
 
 
 def matmul(a, b):
@@ -35,6 +33,18 @@
 
 def matmul_t(a, b):
     return lax.dot_general(a, b, (((1,), (1,)), ((), ())), preferred_element_type=F32)
+
+
+def matmul_halves(a_ref, b):
+    half = a_ref.shape[0] // 2
+    return jnp.concatenate([matmul(a_ref[:half], b), matmul(a_ref[half:], b)], axis=0)
+
+
+def pick(i, values):
+    out = values[-1]
+    for n in range(len(values) - 1):
+        out = jnp.where(i == n, values[n], out)
+    return out
 
 
 def lane_blocks(x):
@@ -53,10 +63,10 @@
 
 
 def kernel(
-    x_hbm, cos_ref, sin_ref, gain_ref, bq_ref, bk_ref, bv_ref, wq_hbm, wk_hbm, wv_hbm, wo_hbm,
+    x_hbm, cos_hbm, sin_hbm, gain_hbm, bq_hbm, bk_hbm, bv_hbm, wq_hbm, wk_hbm, wv_hbm, wo_hbm,
     y_hbm, kc_hbm, vc_hbm,
-    xbuf, hbuf, wkv, wbuf, kv, kst, qbuf, qst, run_max, run_sum, mixed, obuf, ost,
-    xsem, wkvsem, wqsem, wosem, ysem, csem,
+    xbuf, hbuf, cos_half, sin_half, gain_ref, bq_ref, bk_ref, bv_ref, cos_ref, sin_ref, wbuf, kv, kst, qbuf, qst, run_max, run_sum, mixed, obuf, ost, summed,
+    xsem, smallsem, wkvsem, wqsem, wosem, ysem, csem,
     kv_recv, kv_send, q_recv, q_send, o_recv, o_send, fwd_send,
 ):
     me = lax.axis_index("sp")
@@ -86,36 +96,54 @@
     for on_chip, on_core in ((chip, other), (up, core), (up, other), (down, core), (down, other)):
         pl.semaphore_signal(barrier, inc=1, device_id=device(on_chip, on_core), device_id_type=pl.DeviceIdType.MESH)
 
-    first_group = jnp.where(chip == 0, 0, 1)
-
     def group_at(i):
-        return lax.rem(i + first_group, GROUPS)
-
-    def kv_load(chunk_i, kind):
+        return jnp.where(i < 2, 1 - i, i)
+
+    def kv_load(i, kind):
         w_hbm = wk_hbm if kind == 0 else wv_hbm
-        chunk = 2 * chunk_i + kind
-        cols = pl.ds(pl.multiple_of(group_at(chunk_i) * 256, 256), 256)
-        return pltpu.make_async_copy(w_hbm.at[:, cols], wkv.at[lax.rem(chunk, 4)], wkvsem.at[chunk])
+        cols = pl.ds(pl.multiple_of(group_at(i) * 256, 256), 256)
+        return pltpu.make_async_copy(
+            w_hbm.at[:, cols], wbuf.at[i, :, kind * 256 : (kind + 1) * 256], wkvsem.at[i, kind])
 
     def wide_load(w_hbm, g, sem):
         cols = pl.ds(pl.multiple_of(g * 768, 256), 768)
         return pltpu.make_async_copy(w_hbm.at[:, cols], wbuf.at[g], sem.at[g])
 
-    x_copy = pltpu.make_async_copy(x_hbm, xbuf, xsem)
-    x_copy.start()
-    for i in range(2):
-        for kind in range(2):
-            kv_load(jnp.int32(i), kind).start()
-    x_copy.wait()
-
-    @pl.loop(0, tokens // 32)
-    def _(i):
-        rows = pl.ds(pl.multiple_of(i * 32, 32), 32)
-        wide = xbuf[rows, :].astype(F32)
-        inv_rms = lax.rsqrt(jnp.mean(wide * wide, axis=-1, keepdims=True) + NORM_EPS)
-        hbuf[rows, :] = (wide * inv_rms * gain_ref[...]).astype(BF16)
-
-    pl.semaphore_wait(barrier, 5)
+    def x_copy(n):
+        rows = pl.ds(n * (tokens // 4), tokens // 4)
+        return pltpu.make_async_copy(x_hbm.at[rows], xbuf.at[rows], xsem.at[n])
+
+    small_copies = [
+        pltpu.make_async_copy(src, dst, smallsem.at[n])
+        for n, (src, dst) in enumerate((
+            (gain_hbm, gain_ref), (bk_hbm, bk_ref), (bv_hbm, bv_ref), (bq_hbm, bq_ref), (cos_hbm, cos_half), (sin_hbm, sin_half)))
+    ]
+    x_copy(0).start()
+    small_copies[0].start()
+    for n in range(1, 4):
+        x_copy(n).start()
+    for copy in small_copies[1:]:
+        copy.start()
+    small_copies[0].wait()
+    gain = gain_ref[...].astype(F32)[None]
+    for n in range(4):
+        with jax.named_scope("x_wait"):
+            x_copy(n).wait()
+        if n == 1:
+            for i in range(GROUPS):
+                for kind in range(2):
+                    kv_load(jnp.int32(i), kind).start()
+        for start in range(n * (tokens // 4), (n + 1) * (tokens // 4), 32):
+            wide = xbuf[start : start + 32, :].astype(F32)
+            inv_rms = lax.rsqrt(jnp.mean(wide * wide, axis=-1, keepdims=True) + NORM_EPS)
+            hbuf[start : start + 32, :] = (wide * inv_rms * gain).astype(BF16)
+
+    for copy in small_copies[1:]:
+        copy.wait()
+    cos_ref[...] = jnp.concatenate([cos_half[...], cos_half[...]], axis=1)
+    sin_ref[...] = jnp.concatenate([-sin_half[...], sin_half[...]], axis=1)
+    with jax.named_scope("entry"):
+        pl.semaphore_wait(barrier, 5)
 
     def rope(u):
         wide = u.astype(F32)
@@ -125,19 +153,26 @@
         return jnp.logical_not((chip == 3) & (g == 0))
 
     def goes_up(g):
-        return (chip <= 1) | ((chip == 2) & (g >= 1)) | ((chip == 3) & (g <= 1))
+        return (chip <= 1) | ((chip == 2) & (g >= 1)) | ((chip == 3) & (g == 0))
 
     def goes_down(g):
-        return ((chip == 0) & (g >= 1)) | ((chip == 1) & ((g == 0) | (g == 3))) | ((chip == 2) & (g <= 1)) | ((chip == 3) & (g == 2))
+        return ((chip == 0) & (g >= 1)) | ((chip == 1) & ((g == 0) | (g == 3))) | ((chip == 2) & ((g == 0) | (g == 2))) | ((chip == 3) & (g == 2))
+
+    def own_pair(g, first, on_chip):
+        dst = kv.at[chip, g, :, my_rows, :]
+        recv = kv_recv.at[chip, g, core]
+        return [
+            remote(dst, dst, kv_send.at[g, first], recv, on_chip, core),
+            remote(kst.at[g], dst, kv_send.at[g, first + 1], recv, on_chip, other)]
 
     def own_copies(g):
         dst = kv.at[chip, g, :, my_rows, :]
-        recv = kv_recv.at[chip, g, core]
-        yield goes_partner(g), [remote(kst.at[g], dst, kv_send.at[g, 0], recv, chip, other)]
-        yield goes_up(g), [
-            remote(dst, dst, kv_send.at[g, 1], recv, up, core), remote(kst.at[g], dst, kv_send.at[g, 2], recv, up, other)]
-        yield goes_down(g), [
-            remote(dst, dst, kv_send.at[g, 3], recv, down, core), remote(kst.at[g], dst, kv_send.at[g, 4], recv, down, other)]
+        yield goes_partner(g), [remote(kst.at[g], dst, kv_send.at[g, 0], kv_recv.at[chip, g, core], chip, other)]
+        yield goes_up(g), own_pair(g, 1, up)
+        yield goes_down(g), own_pair(jnp.where((chip == 2) & (g == 2), 1, g), 3, down)
+
+    def late_copies(g):
+        yield (chip == 3) & (g == 1), own_pair(g, 1, up)
 
     def each(copies, act):
         for go, group in copies:
@@ -150,22 +185,30 @@
     def _(i):
         g = group_at(i)
         cols = pl.ds(pl.multiple_of(g * 256, 256), 256)
-        for kind, b_ref in ((0, bk_ref), (1, bv_ref)):
-            chunk = 2 * i + kind
+        for kind in range(2):
             kv_load(i, kind).wait()
-            u = (matmul(hbuf[...], wkv[lax.rem(chunk, 4)]) + b_ref[:, cols]).astype(BF16)
-            even, odd = lane_blocks(u)
-            if kind == 0:
-                even, odd = rope(even), rope(odd)
-            kv[chip, g, kind, my_rows, :] = jnp.where(core == 0, even, odd)
-            kst[g, kind] = jnp.where(core == 0, odd, even)
-
-            @pl.when(i < 2)
-            def _():
-                kv_load(i + 2, kind).start()
+        with jax.named_scope("kv_proj"):
+            for kind, b_ref in ((0, bk_ref), (1, bv_ref)):
+                u = (matmul(hbuf[...], wbuf[i, :, kind * 256 : (kind + 1) * 256]) + b_ref[cols].astype(F32)[None]).astype(BF16)
+                even, odd = lane_blocks(u)
+                if kind == 0:
+                    even, odd = rope(even), rope(odd)
+                kv[chip, g, kind, my_rows, :] = jnp.where(core == 0, even, odd)
+                kst[g, kind] = jnp.where(core == 0, odd, even)
 
         wide_load(wq_hbm, i, wqsem).start()
         each(own_copies(g), lambda copy: copy.start())
+
+    def wait_straight(s, g):
+        for j in range(2):
+            part = kv.at[s, g, :, pl.ds(j * tokens, tokens), :]
+            pltpu.make_async_copy(part, part, kv_recv.at[s, g, j]).wait()
+
+    def wait_passed(s, g):
+        pltpu.make_async_copy(kv.at[s, g], kv.at[s, g], kv_recv.at[s, g, 0]).wait()
+
+    def pass_on(s, g, to_chip, slot):
+        return remote(kv.at[s, g], kv.at[s, g], fwd_send.at[slot], kv_recv.at[s, g, 0], to_chip, core)
 
     def q_copies(g):
         mine = qbuf.at[g, :, my_rows, :]
@@ -179,29 +222,38 @@
 
     @pl.loop(0, GROUPS)
     def _(g):
-        wide_load(wq_hbm, g, wqsem).wait()
-        heads = []
-        for n in range(3):
-            cols = pl.ds(pl.multiple_of(g * 768 + n * 256, 256), 256)
-            u = (matmul(hbuf[...], wbuf[g, :, n * 256 : (n + 1) * 256]) + bq_ref[:, cols]).astype(BF16)
-            heads += [rope(part) for part in lane_blocks(u)]
-        for r in range(REPS):
-            even, odd = heads[r], heads[REPS + r]
-            qbuf[g, r, my_rows, :] = jnp.where(core == 0, even, odd)
-            qst[g, r] = jnp.where(core == 0, odd, even)
+        @pl.when(g == GROUPS - 1)
+        def _():
+            @pl.when(chip == 1)
+            def _():
+                wait_straight(2, 0)
+                pass_on(2, 0, 0, 1).start()
+
+            @pl.when(chip == 2)
+            def _():
+                wait_straight(1, 1)
+                pass_on(1, 1, 3, 0).start()
+
+            @pl.when(chip == 3)
+            def _():
+                wait_straight(0, 1)
+                pass_on(0, 1, 2, 0).start()
+
+        with jax.named_scope("q_wait"):
+            wide_load(wq_hbm, g, wqsem).wait()
+        with jax.named_scope("q_proj"):
+            heads = []
+            for n in range(3):
+                cols = pl.ds(pl.multiple_of(g * 768 + n * 256, 256), 256)
+                u = (matmul_halves(hbuf, wbuf[g, :, n * 256 : (n + 1) * 256]) + bq_ref[cols].astype(F32)[None]).astype(BF16)
+                heads += [rope(part) for part in lane_blocks(u)]
+            for r in range(REPS):
+                even, odd = heads[r], heads[REPS + r]
+                qbuf[g, r, my_rows, :] = jnp.where(core == 0, even, odd)
+                qst[g, r] = jnp.where(core == 0, odd, even)
         wide_load(wo_hbm, g, wosem).start()
         each(q_copies(g), lambda copy: copy.start())
-
-    def wait_straight(s, g):
-        for j in range(2):
-            part = kv.at[s, g, :, pl.ds(j * tokens, tokens), :]
-            pltpu.make_async_copy(part, part, kv_recv.at[s, g, j]).wait()
-
-    def wait_passed(s, g):
-        pltpu.make_async_copy(kv.at[s, g], kv.at[s, g], kv_recv.at[s, g, 0]).wait()
-
-    def pass_on(s, g, to_chip, slot):
-        return remote(kv.at[s, g], kv.at[s, g], fwd_send.at[slot], kv_recv.at[s, g, 0], to_chip, core)
+        each(late_copies(g), lambda copy: copy.start())
 
     q_tiles = block // TILE
 
@@ -294,80 +346,100 @@
         def _():
             wait_straight(1, 3)
             pass_on(1, 3, 3, 0).start()
-            wait_straight(3, 1)
-            pass_on(3, 1, 1, 1).start()
             wait_straight(3, 0)
             for j in range(2):
                 part = qbuf.at[GROUPS, :, pl.ds(j * tokens, tokens), :]
                 pltpu.make_async_copy(part, part, q_recv.at[GROUPS, j]).wait()
 
-        masked_item(i, g, jnp.where(i == GROUPS, 3, chip), g)
+        with jax.named_scope('masked'):
+            masked_item(i, g, jnp.where(i == GROUPS, 3, chip), g)
 
         @pl.when((chip == 0) & (i < GROUPS))
         def _():
             finish(i)
 
-    straight = jnp.where(chip == 0, 3, jnp.where(chip == 3, 6, 4))
-    items = straight + jnp.where(chip == 3, 3, jnp.where(chip == 2, 4, 0))
-
-    @pl.loop(0, items)
+    def wait_o(g, parity):
+        part = obuf.at[:, head_cols(g, parity)]
+        pltpu.make_async_copy(part, part, o_recv.at[g, parity]).wait()
+
+    def out_parts(n):
+        for part in range(3):
+            yield part, pl.ds(pl.multiple_of(n * 768 + part * 256, 256), 256)
+
+    def out_product(n, part, g):
+        weight = wbuf[n, g * 768 : (g + 1) * 768, part * 256 : (part + 1) * 256]
+        return matmul_halves(obuf.at[:, g * 768 : (g + 1) * 768], weight)
+
+    tables = (
+        ((0, 1, 2, 4), (0, 0, 0, 0)),
+        ((0, 0, 0, 0, 4), (1, 0, 2, 3, 0)),
+        ((1, 1, 0, 1, 0, 1, 0, 4, 0), (1, 0, 1, 2, 2, 3, 3, 0, 0)),
+        ((0, 2, 0, 0, 2, 2, 1, 1, 4, 1), (2, 1, 1, 3, 2, 3, 1, 3, 0, 2)),
+    )
+
+    @pl.loop(0, pick(chip, [len(sources) for sources, _ in tables]))
     def _(i):
-        late = i - straight
-        in_order = lax.rem(i, GROUPS)
-        shifted = lax.rem(i + 1, GROUPS)
-        s = jnp.where(
-            chip == 0, i,
-            jnp.where(chip == 1, 0,
-                jnp.where(chip == 2, jnp.where(late < 0, 1, 0), jnp.where(late < 0, 2 - 2 * lax.rem(i, 2), 1))))
-        g = jnp.where(
-            chip == 0, 0,
-            jnp.where(chip == 1, in_order,
-                jnp.where(chip == 2, shifted, jnp.where(late < 0, 1 + lax.div(i, 2), 1 + lax.rem(2 * late + 6, 3)))))
-        q_slot = jnp.where(chip == 0, GROUPS, g)
-        is_passed = ((chip == 0) & (i == 2)) | (late >= 0)
-        is_local = (chip == 0) & (i == 0)
-
-        @pl.when(is_passed)
-        def _():
-            wait_passed(s, g)
-
-        @pl.when(jnp.logical_not(is_passed | is_local))
-        def _():
-            wait_straight(s, g)
-
-        @pl.when((chip == 1) & (i == 0))
-        def _():
-            pass_on(0, 0, 2, 0).start()
-
-        @pl.when((chip == 1) & (i == 1))
-        def _():
-            wait_straight(2, 0)
-            pass_on(2, 0, 0, 1).start()
-
-        @pl.when((chip == 2) & (late < 0) & ((g == 1) | (g == 2)))
-        def _():
-            pass_on(1, g, 3, g - 1).start()
-
-        @pl.when((chip == 3) & (late < 0) & (s == 0))
-        def _():
-            pass_on(0, g, 2, g - 1).start()
-
-        full_item(q_slot, g, s, g)
-
-    @pl.when(chip == 0)
-    def _():
-        for j in range(2):
-            rows = pl.ds(j * tokens, tokens)
-            for r in range(REPS):
-                ost[GROUPS + j, :, r * 128 : (r + 1) * 128] = normalized(0, r, rows)
-        for copy in back_copies():
-            copy.start()
-
-    @pl.when(chip > 0)
-    def _():
-        @pl.loop(low, GROUPS)
-        def _(g):
-            finish(g)
+        s = pick(chip, [pick(i, sources) for sources, _ in tables])
+        g = pick(chip, [pick(i, groups) for _, groups in tables])
+        @pl.when(s < CHIPS)
+        def _():
+            q_slot = jnp.where(chip == 0, GROUPS, g)
+            is_passed = ((chip == 0) & (s == 2)) | ((chip == 2) & (s == 0)) | ((chip == 3) & (s == 1))
+            is_here = ((chip == 0) & (s == 0)) | ((chip == 2) & (s == 1) & (g == 1)) | ((chip == 3) & (s == 0) & (g == 1))
+
+            with jax.named_scope("item_wait"):
+                @pl.when(is_passed)
+                def _():
+                    wait_passed(s, g)
+
+                @pl.when(jnp.logical_not(is_passed | is_here))
+                def _():
+                    wait_straight(s, g)
+
+            @pl.when((chip == 0) & (s == 2))
+            def _():
+                wait_straight(3, 1)
+                pass_on(3, 1, 1, 1).start()
+
+            @pl.when((chip == 1) & (g == 0))
+            def _():
+                pass_on(0, 0, 2, 0).start()
+
+            @pl.when((chip == 2) & (s == 1) & (g == 2))
+            def _():
+                pass_on(1, 2, 3, 1).start()
+
+            @pl.when((chip == 3) & (s == 0) & (g >= 2))
+            def _():
+                pass_on(0, g, 2, g - 1).start()
+
+            with jax.named_scope('full'):
+                full_item(q_slot, g, s, g)
+
+            @pl.when((chip == 1) | ((chip == 2) & (s == 0)) | ((chip == 3) & (s == 1)))
+            def _():
+                finish(g)
+
+            @pl.when((chip == 0) & (s == 2))
+            def _():
+                for j in range(2):
+                    rows = pl.ds(j * tokens, tokens)
+                    for r in range(REPS):
+                        ost[GROUPS + j, :, r * 128 : (r + 1) * 128] = normalized(0, r, rows)
+                for copy in back_copies():
+                    copy.start()
+
+        @pl.when(s == CHIPS)
+        def _():
+            wait_o(1, other)
+            wait_o(3, other)
+
+            @pl.loop(0, 4)
+            def _(n):
+                wide_load(wo_hbm, n, wosem).wait()
+                with jax.named_scope("o_proj_a"):
+                    for part, cols in out_parts(n):
+                        summed[:, cols] = xbuf[:, cols].astype(F32) + (out_product(n, part, 1) + out_product(n, part, 3))
 
     @pl.when(chip == 1)
     def _():
@@ -386,18 +458,17 @@
     for copy in cache_copies:
         copy.start()
 
-    def wait_o(g, parity):
-        part = obuf.at[:, head_cols(g, parity)]
-        pltpu.make_async_copy(part, part, o_recv.at[g, parity]).wait()
-
-    @pl.loop(low, GROUPS)
-    def _(g):
-        wait_o(g, other)
-
-    @pl.when(chip == 3)
-    def _():
-        for parity in range(2):
-            wait_o(0, parity)
+    with jax.named_scope("o_wait"):
+        wait_o(2, other)
+
+        @pl.when(chip < 3)
+        def _():
+            wait_o(0, other)
+
+        @pl.when(chip == 3)
+        def _():
+            for parity in range(2):
+                wait_o(0, parity)
 
     def y_copy(n):
         cols = pl.ds(pl.multiple_of(n * 768, 256), 768)
@@ -405,17 +476,16 @@
 
     @pl.loop(0, 4)
     def _(n):
-        wide_load(wo_hbm, n, wosem).wait()
-        for part in range(3):
-            cols = pl.ds(pl.multiple_of(n * 768 + part * 256, 256), 256)
-            summed = matmul(obuf[...], wbuf[n, :, part * 256 : (part + 1) * 256])
-            xbuf[:, cols] = (xbuf[:, cols].astype(F32) + summed).astype(BF16)
+        with jax.named_scope("o_proj"):
+            for part, cols in out_parts(n):
+                xbuf[:, cols] = (summed[:, cols] + (out_product(n, part, 0) + out_product(n, part, 2))).astype(BF16)
         y_copy(n).start()
 
     @pl.loop(0, GROUPS)
     def _(g):
         each(own_copies(g), lambda copy: copy.wait_send())
         each(q_copies(g), lambda copy: copy.wait_send())
+        each(late_copies(g), lambda copy: copy.wait_send())
 
     @pl.loop(low, GROUPS)
     def _(g):
@@ -439,6 +509,28 @@
     @pl.loop(0, 4)
     def _(n):
         y_copy(n).wait()
+
+
+def hand_over(*refs):
+    count = len(refs) // 3
+    sources, targets, buffers = refs[:count], refs[count : 2 * count], refs[2 * count : 3 * count]
+    in_sem, out_sem = refs[3 * count :]
+    pieces = []
+    for n in range(count):
+        rows = sources[n].shape[0] // 4
+        for part in range(4):
+            at = pl.ds(part * rows, rows)
+            slot = len(pieces)
+            pieces.append((
+                pltpu.make_async_copy(sources[n].at[at], buffers[n].at[at], in_sem.at[slot]),
+                pltpu.make_async_copy(buffers[n].at[at], targets[n].at[at], out_sem.at[slot])))
+    for load, _ in pieces:
+        load.start()
+    for load, store in pieces:
+        load.wait()
+        store.start()
+    for _, store in pieces:
+        store.wait()
 
 
 def solution(mesh):
@@ -453,7 +545,7 @@
         block = 2 * tokens
         seq_len = tokens * group_size
         cosine, sine = rope_tables(positions)
-        vmem = pl.BlockSpec(memory_space=pltpu.VMEM)
+        small = (norm_gain, b_q, b_k, b_v)
         anywhere = pl.BlockSpec(memory_space=pl.ANY)
         dma = pltpu.SemaphoreType.DMA
         y, keys, values = pl.pallas_call(
@@ -463,12 +555,16 @@
                 jax.ShapeDtypeStruct((seq_len, HEAD_DIM), BF16),
                 jax.ShapeDtypeStruct((seq_len, HEAD_DIM), BF16),
             ],
-            in_specs=[anywhere] + [vmem] * 6 + [anywhere] * 4,
+            in_specs=[anywhere] * 11,
             out_specs=[anywhere] * 3,
             scratch_shapes=[
                 pltpu.VMEM((tokens, width), BF16),
                 pltpu.VMEM((tokens, width), BF16),
-                pltpu.VMEM((4, width, 256), BF16),
+                pltpu.VMEM((tokens, HEAD_DIM // 2), F32),
+                pltpu.VMEM((tokens, HEAD_DIM // 2), F32),
+                *(pltpu.VMEM(a.shape, BF16) for a in small),
+                pltpu.VMEM((tokens, HEAD_DIM), F32),
+                pltpu.VMEM((tokens, HEAD_DIM), F32),
                 pltpu.VMEM((GROUPS, width, 768), BF16),
                 pltpu.VMEM((CHIPS, GROUPS, 2, block, HEAD_DIM), BF16),
                 pltpu.VMEM((GROUPS, 2, tokens, HEAD_DIM), BF16),
@@ -479,7 +575,8 @@
                 pltpu.VMEM((GROUPS, REPS, block, HEAD_DIM), F32),
                 pltpu.VMEM((tokens, width), BF16),
                 pltpu.VMEM((GROUPS + 2, tokens, REPS * HEAD_DIM), BF16),
-                dma, dma((8,)), dma((4,)), dma((4,)), dma((4,)), dma((CHIPS, 2)),
+                pltpu.VMEM((tokens, width), F32),
+                dma((4,)), dma((6,)), dma((GROUPS, 2)), dma((4,)), dma((4,)), dma((4,)), dma((CHIPS, 2)),
                 dma((CHIPS, GROUPS, 2)), dma((GROUPS, 5)), dma((GROUPS + 1, 2)), dma((GROUPS, 2)),
                 dma((GROUPS, 2)), dma((GROUPS + 2,)), dma((3,)),
             ],
@@ -487,9 +584,17 @@
                 collective_id=0, has_side_effects=True, vmem_limit_bytes=67043328),
             name="block",
         )(
-            hidden, cosine, sine, norm_gain.astype(F32)[None], b_q.astype(F32)[None], b_k.astype(F32)[None],
-            b_v.astype(F32)[None], w_q, w_k, w_v, w_o,
+            hidden, cosine, sine, *small, w_q, w_k, w_v, w_o,
         )
+        results = (y, keys, values)
+        y, keys, values = pl.pallas_call(
+            hand_over,
+            out_shape=[jax.ShapeDtypeStruct(a.shape, a.dtype) for a in results],
+            in_specs=[anywhere] * 3,
+            out_specs=[anywhere] * 3,
+            scratch_shapes=[pltpu.VMEM(a.shape, a.dtype) for a in results] + [dma((12,)), dma((12,))],
+            name="hand_over",
+        )(*results)
         return y, keys[:, None, :], values[:, None, :]
 
     return jax.shard_map(local, mesh=mesh, in_specs=(row_spec, pos_spec, whole, whole, whole, whole, whole, whole, whole, whole), out_specs=(row_spec, cache_spec, cache_spec), check_vma=False)

time: 95 us -> 69.3 us (0.73)
  the two profiles are of different devices: /device:TPU:125 before, /device:TPU:86 now
where the time goes in v2:
time: 69.3 us; the launch traced here: 69.1 us
  Pallas kernels  66.1 us (95%)
  other arithmetic  2.2 us (3%)
  between operations  0.8 us (1%)
    pallas_call x1, Pallas kernels, local(): pl.pallas_call(kernel, out_shape=[jax.ShapeDtypeStruct((tokens, width), B...  62.9 us
    pallas_call x1, Pallas kernels, local(): pl.pallas_call(hand_over, out_shape=[jax.ShapeDtypeStruct(a.shape, a.dtyp...  3.2 us
    sin x1, other arithmetic, rope_tables(): return (jnp.cos(angle), jnp.sin(angle))  1.5 us

profile of v2, /device:TPU:86, one launch (start us, length us, event | category | flops | bytes accessed | tf_op | source)
XLA Modules:
  0.0 69.1 jit_solution(7226069077683079821)
XLA Ops:
  0.6 0.7 convert_element_type.3
  1.3 1.5 %multiply_sine_fusion = (f32[384,64]{1,0:T(8,128)}, f32[384,64]{1,0:T(8,128)}) fusion(f32[64]{0:T(128)S(1)} %multiply_power_fusion, f32[384]{0:T(512)S(1)} %convert_element_type.3), kind=kLoop, calls=%fused_computation | loop fusion | flops 24576 | bytes 198400 | tf_op jit(solution)/shard_map/sin | solution.py:27
  2.8 62.9 %block.1 = (bf16[384,3072]{1,0:T(8,128)(2,1)}, bf16[3072,128]{1,0:T(8,128)(2,1)}, bf16[3072,128]{1,0:T(8,128)(2,1)}) custom-call(bf16[384,3072]{1,0:T(8,128)(2,1)} %x_hbm.1, f32[384,64]{1,0:T(8,128)} %get-tuple-element.16.cos_hbm, f32[384,64]{1,0:T(8,128)} %get-tuple-element.15.sin_hbm, bf16[3072]{0:T(1024)(128)(2,1)} %gain_hbm.1, bf16[3072]{0:T(1024)(128)(2,1)} %bq_hbm.1, ...), custom_call_target="tpu_custom_call" | custom-call | tf_op jit(solution)/shard_map/block/pallas_call | solution.py:551
  65.8 3.2 %hand_over.1 = (bf16[384,3072]{1,0:T(8,128)(2,1)}, bf16[3072,128]{1,0:T(8,128)(2,1)}, bf16[3072,128]{1,0:T(8,128)(2,1)}) custom-call(bf16[384,3072]{1,0:T(8,128)(2,1)} %get-tuple-element.9.refs_0_, bf16[3072,128]{1,0:T(8,128)(2,1)} %get-tuple-element.10.refs_1_, bf16[3072,128]{1,0:T(8,128)(2,1)} %get-tuple-element.11.refs_2_), custom_call_target="tpu_custom_call" | custom-call | tf_op jit(solution)/shard_map/hand_over/pallas_call | solution.py:590
  (1 shorter events, 0.0 us)
